TPU v7x, 32 devices: a whole 2x2x4 slice. The times are simulated.
32 devices in a mesh: fsdp: 4 (over y, x), rep: 8 (over z, core).
Axes of the slice: x: 2, y: 2, z: 4, core: 2. Of those that a mesh axis runs over, the one named last changes fastest.
Arguments:
- hidden_in: bfloat16 [8192, 2048], P(('fsdp', 'rep'))
- out_grad: bfloat16 [8192, 2048], P(('fsdp', 'rep')), may hold values from -6 to 6
- attn_saved: bfloat16 [8192, 256], P(('fsdp', 'rep')), may hold values from -6 to 6
- row_lse: float32 [8192, 2], P(('fsdp', 'rep')), may hold values from 2.5 to 6
- w_qkv: bfloat16 [2048, 512], P('fsdp'), may hold values from -0.125 to 0.125
- w_out_t: bfloat16 [2048, 256], P('fsdp'), may hold values from -0.125 to 0.125
- doc_lengths: int32 [32, 4], P(('fsdp', 'rep')), may hold values from 1 to 128, 256 in all within a row
- seq_start: int32 [32], P(('fsdp', 'rep')), may hold values from 0 to 2047
Outputs:
- input_grad: bfloat16 [8192, 2048], P(('fsdp', 'rep'))
- grad_update: float32 [2048, 768], P('fsdp')
- grad_norm: float32 [], replicated
Inputs may be any that keep to these rules, and one draw needn't show every extreme that they name: `doc_lengths`: each row sums to 256; the longest document of each device has exactly 128 tokens.
All inputs are finite; a program needn't handle non-finite values.
Results may differ from a plain program's by a relative error of at most 0.014.
Values may be sent and summed in bfloat16 or wider, within the bound.
A program may use at most 64 MiB of HBM per device.

v0:
```python
import jax
import jax.numpy as jnp
from jax import lax
from jax.sharding import PartitionSpec as P

D = 2048
HEAD = 128


def rotary(values_in, positions, turn, head_size):
    rows = values_in.shape[0]
    heads_count = values_in.shape[1] // head_size
    half_size = head_size // 2
    inverse = 1000000.0 ** (-(jnp.arange(half_size, dtype=jnp.float32) * 2.0) / head_size)
    angles = positions.astype(jnp.float32)[:, None] * inverse[None, :]
    cosine = jnp.cos(angles)[:, None, :]
    sines = jnp.sin(angles)[:, None, :]
    shaped = values_in.reshape(rows, heads_count, head_size)
    first_half = shaped[:, :, :half_size]
    second_half = shaped[:, :, half_size:]
    result = jnp.concatenate(
        [
            first_half * cosine - turn * second_half * sines,
            second_half * cosine + turn * first_half * sines,
        ],
        axis=2,
    )
    return result.reshape(rows, heads_count * head_size)


def contract_rows(left, right):
    return lax.dot_general(
        left, right, (((0,), (0,)), ((), ())), preferred_element_type=jnp.float32
    )


def contract_cols(left, right):
    return lax.dot_general(
        left, right, (((1,), (1,)), ((), ())), preferred_element_type=jnp.float32
    )


def body(hidden_in, out_grad, attn_saved, row_lse, w_qkv, w_out_t, doc_lengths, seq_start):
    seq_rows = hidden_in.shape[0]
    head_size = HEAD
    query_width = attn_saved.shape[1]
    heads_count = row_lse.shape[1]
    scale = 1.0 / head_size**0.5
    tokens_part = hidden_in
    grads_part = out_grad
    proj = jnp.dot(
        tokens_part,
        lax.all_gather(w_qkv, "fsdp", axis=0, tiled=True),
        preferred_element_type=jnp.float32,
    )
    attn_full = jnp.dot(
        grads_part,
        lax.all_gather(w_out_t, "fsdp", axis=0, tiled=True),
        preferred_element_type=jnp.float32,
    )
    attn_grad = attn_full.astype(jnp.bfloat16)
    positions = seq_start[0] + jnp.arange(seq_rows, dtype=jnp.int32)
    queries = rotary(proj[:, :query_width], positions, 1.0, head_size).astype(jnp.bfloat16)
    keys = rotary(proj[:, query_width : query_width + head_size], positions, 1.0, head_size).astype(
        jnp.bfloat16
    )
    values_all = proj[:, query_width + head_size :].astype(jnp.bfloat16)
    ends = jnp.cumsum(doc_lengths[0])
    local_rows = jnp.arange(seq_rows, dtype=jnp.int32)
    documents = jnp.sum((local_rows[:, None] >= ends[None, :]).astype(jnp.int32), axis=1)
    block_rows = min(seq_rows, 512)
    block_count = seq_rows // block_rows

    def attend_block(carry, inputs):
        key_grad, value_grad = carry
        query_rows, grad_rows, saved_rows, lse_rows, index_rows, doc_rows = inputs
        allowed = (doc_rows[:, None] == documents[None, :]) & (
            local_rows[None, :] <= index_rows[:, None]
        )
        query_parts = []
        for head_index in range(heads_count):
            lower = head_index * head_size
            query_head = query_rows[:, lower : lower + head_size]
            scores = contract_cols(query_head, keys) * scale
            probs = jnp.where(
                allowed, jnp.exp(scores - lse_rows[:, head_index : head_index + 1]), 0.0
            )
            grad_head = grad_rows[:, lower : lower + head_size]
            dprobs = contract_cols(grad_head, values_all)
            delta = jnp.sum(
                grad_head.astype(jnp.float32)
                * saved_rows[:, lower : lower + head_size].astype(jnp.float32),
                axis=1,
                keepdims=True,
            )
            dscores = (probs * (dprobs - delta) * scale).astype(jnp.bfloat16)
            probs_low = probs.astype(jnp.bfloat16)
            value_grad = value_grad + contract_rows(probs_low, grad_head)
            query_parts.append(jnp.dot(dscores, keys, preferred_element_type=jnp.float32))
            key_grad = key_grad + contract_rows(dscores, query_head)
        return ((key_grad, value_grad), jnp.concatenate(query_parts, axis=1))

    block_inputs = (
        queries.reshape(block_count, block_rows, query_width),
        attn_grad.reshape(block_count, block_rows, query_width),
        attn_saved.reshape(block_count, block_rows, query_width),
        row_lse.reshape(block_count, block_rows, heads_count),
        local_rows.reshape(block_count, block_rows),
        documents.reshape(block_count, block_rows),
    )
    zero_grad = jnp.zeros((seq_rows, head_size), jnp.float32)
    (key_grad, value_grad), query_blocks = lax.scan(
        attend_block, (zero_grad, zero_grad), block_inputs
    )
    query_grad = rotary(
        query_blocks.reshape(seq_rows, query_width), positions, -1.0, head_size
    ).astype(jnp.bfloat16)
    key_grad = rotary(key_grad, positions, -1.0, head_size).astype(jnp.bfloat16)
    d_qkv = jnp.concatenate([query_grad, key_grad, value_grad.astype(jnp.bfloat16)], axis=1)
    input_full = contract_cols(d_qkv, lax.all_gather(w_qkv, "fsdp", axis=0, tiled=True))
    input_grad = input_full.astype(jnp.bfloat16)
    tokens_part = hidden_in
    grads_part = out_grad
    shard_sum = lax.psum_scatter(
        jnp.concatenate(
            [contract_rows(tokens_part, d_qkv), contract_rows(grads_part, attn_saved)], axis=1
        ).astype(jnp.bfloat16),
        "fsdp",
        scatter_dimension=0,
        tiled=True,
    ).astype(jnp.float32)
    grads = lax.psum(shard_sum, "rep")
    norm_sq = lax.psum(jnp.sum(grads * grads), "fsdp")
    grad_update = grads * lax.rsqrt(norm_sq / (D * grads.shape[1]) + 1e-06)
    return (input_grad, grad_update, jnp.sqrt(norm_sq))


def solution(mesh):
    in_specs = (
        P(("fsdp", "rep"), None),
        P(("fsdp", "rep"), None),
        P(("fsdp", "rep"), None),
        P(("fsdp", "rep"), None),
        P("fsdp", None),
        P("fsdp", None),
        P(("fsdp", "rep"), None),
        P(("fsdp", "rep")),
    )
    out_specs = (P(("fsdp", "rep"), None), P("fsdp", None), P())
    return jax.shard_map(body, mesh=mesh, in_specs=in_specs, out_specs=out_specs, check_vma=False)
```

profile of v0, /device:TPU:0, one launch (start us, length us, event | category | flops | bytes accessed | tf_op | source)
XLA Modules:
  0.0 219.8 jit_solution(17886597577698370556)
XLA Ops:
  7.2 0.0 copy-start
  7.2 0.0 copy-start.1
  7.2 0.0 all-gather.5.cloned.1.call-start
  7.2 0.7 all-gather.5.cloned.1.call-update
  7.9 0.0 all-gather.3.cloned.1.call-start
  8.0 0.7 all-gather.3.cloned.1.call-update
  8.7 0.0 reduce-scatter.2.cloned.1.call-start
  9.4 0.9 fusion.49
  10.3 0.7 copy.36
  11.0 0.7 copy.37
  11.7 0.8 reduce-window.8
  12.6 0.7 convert_reduce_fusion
  13.2 1.3 fusion.50
  14.6 1.2 broadcast_multiply_fusion.1
  15.8 0.0 copy-done.1
  15.8 1.4 convolution_convert_fusion.2
  17.2 21.9 %all-gather.5.cloned.1.call-done = bf16[2048,256]{1,0:T(8,128)(2,1)} async-done(((bf16[512,256]{1,0:T(8,128)(2,1)}), bf16[2048,256]{1,0:T(8,128)(2,1)}) %all-gather.5.cloned.1.call-update) | async-done | bytes 1048592 | tf_op jit(solution)/shard_map/all_gather | solution.py:58
  39.1 1.7 convolution_convert_fusion.3
  40.8 0.9 multiply_reduce_fusion.1
  41.8 34.4 %all-gather.3.cloned.1.call-done = bf16[2048,512]{1,0:T(8,128)(2,1)} async-done(((bf16[512,512]{1,0:T(8,128)(2,1)}), bf16[2048,512]{1,0:T(8,128)(2,1)}) %all-gather.3.cloned.1.call-update) | async-done | bytes 2097168 | tf_op jit(solution)/shard_map/all_gather | solution.py:53
  76.1 0.0 copy-done
  76.1 2.3 %fusion.51 = f32[256,512]{1,0:T(8,128)S(1)} fusion(bf16[256,2048]{1,0:T(8,128)(2,1)S(1)} %copy-done, bf16[2048,512]{1,0:T(8,128)(2,1)} %all-gather.3.cloned.1.call-done), kind=kOutput, calls=%fused_computation.89 | convolution fusion | flops 536870912 | bytes 3670016 | tf_op jit(solution)/shard_map/dot_general | solution.py:51
  78.5 0.1 copy.35
  78.6 1.0 fusion.28
  79.6 0.1 reshape.176
  79.7 0.0 copy-start.2
  79.7 0.0 copy-start.3
  79.7 0.0 copy-start.4
  79.7 0.0 copy-start.5
  79.7 0.5 subtract_convert_fusion.1
  80.2 0.4 pad_maximum_fusion.3
  80.6 1.0 fusion.10
  81.6 0.2 fusion.17
  81.8 0.2 fusion.11
  82.0 0.0 copy-done.2
  82.0 0.0 copy-done.3
  82.0 0.2 fusion.47
  82.2 0.2 fusion.37
  82.4 0.0 copy-done.4
  82.4 0.0 copy-done.5
  82.5 0.2 fusion.5
  82.7 0.2 fusion.12
  82.9 0.2 fusion.46
  83.1 0.2 fusion.14
  83.2 0.1 copy.33
  83.4 0.2 fusion.13
  83.6 0.3 fusion.32
  83.9 0.1 copy.32
  84.1 0.1 copy.39
  84.3 0.1 copy.38
  84.4 1.2 subtract_convert_fusion
  85.6 0.4 pad_maximum_fusion.4
  86.0 0.7 fusion
  86.7 1.9 pad_maximum_fusion
  88.6 0.0 reduce-scatter.2.cloned.1.call-update
  88.7 44.1 %reduce-scatter.2.cloned.1.call-done = bf16[512,768]{0,1:T(8,128)(2,1)} async-done(((bf16[2048,768]{0,1:T(8,128)(2,1)}), bf16[512,768]{0,1:T(8,128)(2,1)}) %reduce-scatter.2.cloned.1.call-update) | async-done | bytes 786448 | tf_op jit(solution)/shard_map/reduce_scatter | solution.py:124
  132.7 59.9 %all-reduce.1 = f32[512,768]{0,1:T(8,128)S(1)} all-reduce(bf16[512,768]{0,1:T(8,128)(2,1)} %reduce-scatter.2.cloned.1.call-done), channel_id=1, replica_groups=mesh['fsdp'=4,'rep'=8] {'rep'}, use_global_device_ids=true, to_apply=%region_5.6 | all-reduce | flops 393216 | bytes 2359296 | tf_op jit(solution)/shard_map/psum | solution.py:132
  192.6 1.0 multiply_reduce_fusion
  193.6 3.3 %convolution_convert_fusion.1 = bf16[256,2048]{1,0:T(8,128)(2,1)} fusion(bf16[2048,512]{1,0:T(8,128)(2,1)} %all-gather.3.cloned.1.call-done, bf16[256,128]{1,0:T(8,128)(2,1)S(1)} %copy.33, bf16[256,128]{1,0:T(8,128)(2,1)S(1)} %copy.32, bf16[256,256]{1,0:T(8,128)(2,1)S(1)} %bitcast.49), kind=kOutput, calls=%fused_computation.3 | convolution fusion | flops 538181632 | bytes 3407872 | tf_op jit(solution)/shard_map/dot_general | solution.py:38
  196.9 9.5 %psum.15 = f32[]{:T(128)} all-reduce(f32[]{:T(128)} %multiply_reduce_fusion), channel_id=1, replica_groups=mesh['fsdp'=4,'rep'=8] {'fsdp'}, use_global_device_ids=true, to_apply=%region_7.8 | all-reduce | flops 1 | bytes 8 | tf_op jit(solution)/shard_map/psum | solution.py:133
  207.8 1.3 broadcast_multiply_fusion
  209.1 3.0 %copy.34 = f32[512,768]{1,0:T(8,128)} copy(f32[512,768]{0,1:T(8,128)} %broadcast_multiply_fusion) | data formatting | bytes 3145728
  (9 shorter events, 0.1 us)
Async XLA Ops:
  7.2 69.0 %copy-start = (bf16[256,2048]{1,0:T(8,128)(2,1)S(1)}, bf16[256,2048]{1,0:T(8,128)(2,1)}, u32[]{:S(2)}) copy-start(bf16[256,2048]{1,0:T(8,128)(2,1)} %param.8) | copy-start | bytes 3145732
  7.2 8.6 %copy-start.1 = (bf16[256,2048]{1,0:T(8,128)(2,1)S(1)}, bf16[256,2048]{1,0:T(8,128)(2,1)}, u32[]{:S(2)}) copy-start(bf16[256,2048]{1,0:T(8,128)(2,1)} %param.9) | copy-start | bytes 3145732
  7.2 31.9 %all-gather.5.cloned.1.call-start = ((), (), s32[]{:S(2)}) async-start(), calls=%async_computation.2 | async-start | bytes 1310720 | tf_op jit(solution)/shard_map/all_gather | solution.py:58
  7.9 68.2 %all-gather.3.cloned.1.call-start = ((), (), s32[]{:S(2)}) async-start(), calls=%async_computation.1 | async-start | bytes 2621440 | tf_op jit(solution)/shard_map/all_gather | solution.py:53
  8.7 124.0 %reduce-scatter.2.cloned.1.call-start = ((), (), s32[]{:S(2)}) async-start(), calls=%async_computation.3 | async-start | bytes 3932160 | tf_op jit(solution)/shard_map/reduce_scatter | solution.py:124
  79.7 2.3 %copy-start.2 = (bf16[256,1,64]{0,2,1:T(8,128)(2,1)S(1)}, bf16[256,1,64]{0,2,1:T(8,128)(2,1)}, u32[]{:S(2)}) copy-start(bf16[256,1,64]{0,2,1:T(8,128)(2,1)} %get-tuple-element.64) | copy-start | bytes 98308
  79.7 2.3 %copy-start.3 = (bf16[256,1,64]{0,2,1:T(8,128)(2,1)S(1)}, bf16[256,1,64]{0,2,1:T(8,128)(2,1)}, u32[]{:S(2)}) copy-start(bf16[256,1,64]{0,2,1:T(8,128)(2,1)} %get-tuple-element.65) | copy-start | bytes 98308
  79.7 2.7 %copy-start.4 = (f32[256,1]{0,1:T(1,128)S(1)}, f32[256,1]{0,1:T(1,128)}, u32[]{:S(2)}) copy-start(f32[256,1]{0,1:T(1,128)} %get-tuple-element.68) | copy-start | bytes 3076
  79.7 2.7 %copy-start.5 = (s32[256]{0:T(256)S(1)}, s32[256]{0:T(256)}, u32[]{:S(2)}) copy-start(s32[256]{0:T(256)} %convert_reduce_fusion) | copy-start | bytes 3076
Sparse Core Ops, SparseCore 0:
  9.8 29.2 all-gather.4
  40.9 35.1 all-gather.2
  88.8 43.8 reduce-scatter.1
where the time goes:
time: 220 us
  waiting for transfers between devices  102 us (46%)
  blocking collectives  69.4 us (32%)
  between operations  17.2 us (8%)
  matrix products  12.2 us (6%)
  other arithmetic  11.5 us (5%)
  local copies, waits for them, and re-layouts  7.61 us (3%)
    psum x1, blocking collectives, body(): grads = lax.psum(shard_sum, 'rep')  59.9 us
    reduce_scatter x1, waiting for transfers between devices, body(): lax.psum_scatter(jnp.concatenate([contract_rows(tokens_part, d_qkv), cont...  44.1 us
    all_gather x1, waiting for transfers between devices, body(): lax.all_gather(w_qkv, 'fsdp', axis=0, tiled=True)  34.4 us
    all_gather x1, waiting for transfers between devices, body(): lax.all_gather(w_out_t, 'fsdp', axis=0, tiled=True)  21.9 us
    psum x1, blocking collectives, body(): norm_sq = lax.psum(jnp.sum(grads * grads), 'fsdp')  9.53 us
    unnamed x20, local copies, waits for them, and re-layouts  4.97 us
    dot_general x5, matrix products, contract_cols(): lax.dot_general(left, right, (((1,), (1,)), ((), ())), preferred_element_...  4.91 us
  transfers between devices with their start and end apart: 3, of which 3 were waited for; matrix products, arithmetic and copies ran while one was open for 5% of the time, Pallas kernels for 0%

commit v1 on v0

--- a/solution.py
+++ b/solution.py
@@ -5,6 +5,15 @@
 
 D = 2048
 HEAD = 128
+
+
+def add_in_pairs(x, axis):
+    count = lax.axis_size(axis)
+    total, reach = (x, 1)
+    while reach < count:
+        total = total + lax.ppermute(total, axis, [(i, i ^ reach) for i in range(count)])
+        reach = 2 * reach
+    return total
 
 
 def rotary(values_in, positions, turn, head_size):
@@ -129,7 +138,7 @@
         scatter_dimension=0,
         tiled=True,
     ).astype(jnp.float32)
-    grads = lax.psum(shard_sum, "rep")
+    grads = add_in_pairs(shard_sum, "rep")
     norm_sq = lax.psum(jnp.sum(grads * grads), "fsdp")
     grad_update = grads * lax.rsqrt(norm_sq / (D * grads.shape[1]) + 1e-06)
     return (input_grad, grad_update, jnp.sqrt(norm_sq))

time: 220 us -> 269 us (1.22)
  waiting for transfers between devices: 102 us -> 206 us
  blocking collectives: 69.4 us -> 9.54 us
  starting transfers between devices: 0.11 us -> 4.21 us
    ppermute x0 -> x3, waiting for transfers between devices: none -> 104 us  [add_in_pairs(): lax.ppermute(total, axis, [(i, i ^ reach) for i in range(count)])]
    psum x1 -> x0, blocking collectives: 59.9 us -> none  [body(): grads = lax.psum(shard_sum, 'rep')]
    ppermute x0 -> x3, starting transfers between devices: none -> 4.09 us  [add_in_pairs(): lax.ppermute(total, axis, [(i, i ^ reach) for i in range(count)])]
  transfers between devices with their start and end apart: 3 -> 6, of which waited for: 3 -> 6; matrix products, arithmetic and copies ran while one was open for 5% -> 5% of each run, Pallas kernels for 0% -> 0%
where the time goes in v1:
time: 269 us
  waiting for transfers between devices  206 us (77%)
  between operations  17.2 us (6%)
  other arithmetic  13.5 us (5%)
  matrix products  10.6 us (4%)
  blocking collectives  9.54 us (4%)
  local copies, waits for them, and re-layouts  7.62 us (3%)
  starting transfers between devices  4.21 us (2%)
    ppermute x3, waiting for transfers between devices, add_in_pairs(): lax.ppermute(total, axis, [(i, i ^ reach) for i in range(count)])  104 us
    reduce_scatter x1, waiting for transfers between devices, body(): lax.psum_scatter(jnp.concatenate([contract_rows(tokens_part, d_qkv), cont...  44.1 us
    all_gather x1, waiting for transfers between devices, body(): lax.all_gather(w_qkv, 'fsdp', axis=0, tiled=True)  34.4 us
    all_gather x1, waiting for transfers between devices, body(): lax.all_gather(w_out_t, 'fsdp', axis=0, tiled=True)  21.9 us
    psum x1, blocking collectives, body(): norm_sq = lax.psum(jnp.sum(grads * grads), 'fsdp')  9.54 us
  transfers between devices with their start and end apart: 6, of which 6 were waited for; matrix products, arithmetic and copies ran while one was open for 5% of the time, Pallas kernels for 0%

profile of v1, /device:TPU:0, one launch (start us, length us, event | category | flops | bytes accessed | tf_op | source)
XLA Modules:
  0.0 268.9 jit_solution(11960649688716689603)
XLA Ops:
  7.2 0.0 copy-start
  7.2 0.0 all-gather.5.cloned.1.call-start
  7.2 0.7 all-gather.5.cloned.1.call-update
  7.9 0.0 all-gather.3.cloned.1.call-start
  8.0 0.7 all-gather.3.cloned.1.call-update
  8.7 0.0 reduce-scatter.2.cloned.1.call-start
  9.4 0.9 fusion.49
  10.3 0.7 copy.36
  11.0 0.7 copy.37
  11.7 0.8 reduce-window.8
  12.6 0.7 convert_reduce_fusion
  13.2 1.4 fusion.50
  14.6 1.2 broadcast_multiply_fusion.1
  15.8 1.4 convolution_convert_fusion.2
  17.2 21.9 %all-gather.5.cloned.1.call-done = bf16[2048,256]{1,0:T(8,128)(2,1)} async-done(((bf16[512,256]{1,0:T(8,128)(2,1)}), bf16[2048,256]{1,0:T(8,128)(2,1)}) %all-gather.5.cloned.1.call-update) | async-done | bytes 1048592 | tf_op jit(solution)/shard_map/all_gather | solution.py:67
  39.1 1.7 convolution_convert_fusion.3
  40.8 0.9 multiply_reduce_fusion.1
  41.8 34.4 %all-gather.3.cloned.1.call-done = bf16[2048,512]{1,0:T(8,128)(2,1)} async-done(((bf16[512,512]{1,0:T(8,128)(2,1)}), bf16[2048,512]{1,0:T(8,128)(2,1)}) %all-gather.3.cloned.1.call-update) | async-done | bytes 2097168 | tf_op jit(solution)/shard_map/all_gather | solution.py:62
  76.1 0.0 copy-done
  76.1 2.3 fusion.51
  78.5 0.1 copy.35
  78.6 0.9 fusion.28
  79.5 0.1 reshape.176
  79.7 0.0 copy-start.3
  79.7 0.5 subtract_convert_fusion.1
  80.2 0.4 pad_maximum_fusion.3
  80.6 1.0 fusion.10
  81.6 0.2 fusion.17
  81.8 0.2 fusion.11
  82.0 0.0 copy-done.3
  82.0 0.0 copy-done.4
  82.0 0.2 fusion.47
  82.2 0.2 fusion.37
  82.4 0.0 copy-done.5
  82.4 0.2 fusion.5
  82.6 0.2 fusion.12
  82.9 0.2 fusion.46
  83.1 0.2 fusion.14
  83.2 0.1 copy.33
  83.4 0.2 fusion.13
  83.6 0.3 fusion.32
  83.9 0.1 copy.32
  84.1 0.1 copy.39
  84.3 0.1 copy.38
  84.4 1.2 subtract_convert_fusion
  85.6 0.4 pad_maximum_fusion.4
  86.0 0.7 fusion
  86.7 1.9 pad_maximum_fusion
  88.6 0.0 reduce-scatter.2.cloned.1.call-update
  88.6 44.1 %reduce-scatter.2.cloned.1.call-done = bf16[512,768]{0,1:T(8,128)(2,1)} async-done(((bf16[2048,768]{0,1:T(8,128)(2,1)}), bf16[512,768]{0,1:T(8,128)(2,1)}) %reduce-scatter.2.cloned.1.call-update) | async-done | bytes 786448 | tf_op jit(solution)/shard_map/reduce_scatter | solution.py:133
  132.7 1.4 convert_element_type.92
  134.1 0.1 collective-permute-start
  134.2 3.4 %collective-permute-done = f32[512,768]{0,1:T(8,128)S(1)} collective-permute-done((f32[512,768]{0,1:T(8,128)S(1)}, f32[512,768]{0,1:T(8,128)S(1)}, u32[]{:S(2)}, u32[]{:S(2)}) %collective-permute-start) | collective-permute-done | bytes 1572896 | tf_op jit(solution)/shard_map/ppermute | solution.py:14
  137.6 0.2 convert_add_fusion
  137.8 1.6 collective-permute-start.1
  139.4 35.0 %collective-permute-done.1 = f32[512,768]{0,1:T(8,128)S(1)} collective-permute-done((f32[512,768]{0,1:T(8,128)S(1)}, f32[512,768]{0,1:T(8,128)S(1)}, u32[]{:S(2)}, u32[]{:S(2)}) %collective-permute-start.1) | collective-permute-done | bytes 1572896 | tf_op jit(solution)/shard_map/ppermute | solution.py:14
  174.3 0.3 add.61
  174.7 2.5 collective-permute-start.2
  177.2 1.7 convolution_convert_fusion.1
  178.9 66.1 %collective-permute-done.2 = f32[512,768]{0,1:T(8,128)S(1)} collective-permute-done((f32[512,768]{0,1:T(8,128)S(1)}, f32[512,768]{0,1:T(8,128)S(1)}, u32[]{:S(2)}, u32[]{:S(2)}) %collective-permute-start.2) | collective-permute-done | bytes 1572896 | tf_op jit(solution)/shard_map/ppermute | solution.py:14
  244.9 1.1 multiply_reduce_fusion
  246.0 9.5 %psum.7 = f32[]{:T(128)} all-reduce(f32[]{:T(128)} %get-tuple-element.56), channel_id=1, replica_groups=mesh['fsdp'=4,'rep'=8] {'fsdp'}, use_global_device_ids=true, to_apply=%region_6.7 | all-reduce | flops 1 | bytes 8 | tf_op jit(solution)/shard_map/psum | solution.py:142
  256.9 1.3 broadcast_multiply_fusion
  258.2 3.0 %copy.34 = f32[512,768]{1,0:T(8,128)} copy(f32[512,768]{0,1:T(8,128)} %broadcast_multiply_fusion) | data formatting | bytes 3145728
  (19 shorter events, 0.2 us)
Async XLA Ops:
  7.2 69.0 %copy-start = (bf16[256,2048]{1,0:T(8,128)(2,1)S(1)}, bf16[256,2048]{1,0:T(8,128)(2,1)}, u32[]{:S(2)}) copy-start(bf16[256,2048]{1,0:T(8,128)(2,1)} %param.8) | copy-start | bytes 3145732
  7.2 8.6 %copy-start.1 = (bf16[256,2048]{1,0:T(8,128)(2,1)S(1)}, bf16[256,2048]{1,0:T(8,128)(2,1)}, u32[]{:S(2)}) copy-start(bf16[256,2048]{1,0:T(8,128)(2,1)} %param.9) | copy-start | bytes 3145732
  7.2 31.9 %all-gather.5.cloned.1.call-start = ((), (), s32[]{:S(2)}) async-start(), calls=%async_computation.2 | async-start | bytes 1310720 | tf_op jit(solution)/shard_map/all_gather | solution.py:67
  7.9 68.2 %all-gather.3.cloned.1.call-start = ((), (), s32[]{:S(2)}) async-start(), calls=%async_computation.1 | async-start | bytes 2621440 | tf_op jit(solution)/shard_map/all_gather | solution.py:62
  8.7 124.0 %reduce-scatter.2.cloned.1.call-start = ((), (), s32[]{:S(2)}) async-start(), calls=%async_computation.3 | async-start | bytes 3932160 | tf_op jit(solution)/shard_map/reduce_scatter | solution.py:133
  79.7 2.3 copy-start.3
  79.7 2.3 copy-start.4
  79.7 2.7 %copy-start.5 = (f32[256,1]{0,1:T(1,128)S(1)}, f32[256,1]{0,1:T(1,128)}, u32[]{:S(2)}) copy-start(f32[256,1]{0,1:T(1,128)} %get-tuple-element.70) | copy-start | bytes 3076
  79.7 2.7 %copy-start.7 = (s32[256]{0:T(256)S(1)}, s32[256]{0:T(256)}, u32[]{:S(2)}) copy-start(s32[256]{0:T(256)} %convert_reduce_fusion) | copy-start | bytes 3076
  132.7 4.9 %copy-start.2 = (bf16[512,768]{0,1:T(8,128)(2,1)S(1)}, bf16[512,768]{0,1:T(8,128)(2,1)}, u32[]{:S(2)}) copy-start(bf16[512,768]{0,1:T(8,128)(2,1)} %reduce-scatter.2.cloned.1.call-done) | copy-start | bytes 2359300
  134.1 3.5 %collective-permute-start = (f32[512,768]{0,1:T(8,128)S(1)}, f32[512,768]{0,1:T(8,128)S(1)}, u32[]{:S(2)}, u32[]{:S(2)}) collective-permute-start(f32[512,768]{0,1:T(8,128)S(1)} %convert_element_type.92), channel_id=1, source_target_pairs={{0,1},{1,0},{2,3},{3,2},{4,5},{5,4},{6,7},{7,6},{8,9},{9,8},{10,11... | collective-permute-start | bytes 4718600 | tf_op jit(solution)/shard_map/ppermute | solution.py:14
  137.8 39.3 %copy-start.6 = (bf16[2048,512]{1,0:T(8,128)(2,1)S(1)}, bf16[2048,512]{1,0:T(8,128)(2,1)}, u32[]{:S(2)}) copy-start(bf16[2048,512]{1,0:T(8,128)(2,1)} %all-gather.3.cloned.1.call-done) | copy-start | bytes 6291460
  137.8 36.5 %collective-permute-start.1 = (f32[512,768]{0,1:T(8,128)S(1)}, f32[512,768]{0,1:T(8,128)S(1)}, u32[]{:S(2)}, u32[]{:S(2)}) collective-permute-start(f32[512,768]{0,1:T(8,128)S(1)} %convert_add_fusion), channel_id=1, source_target_pairs={{0,2},{1,3},{2,0},{3,1},{4,6},{5,7},{6,4},{7,5},{8,10},{9,11},{10,... | collective-permute-start | bytes 4718600 | tf_op jit(solution)/shard_map/ppermute | solution.py:14
  174.7 70.3 %collective-permute-start.2 = (f32[512,768]{0,1:T(8,128)S(1)}, f32[512,768]{0,1:T(8,128)S(1)}, u32[]{:S(2)}, u32[]{:S(2)}) collective-permute-start(f32[512,768]{0,1:T(8,128)S(1)} %add.61), channel_id=1, source_target_pairs={{0,4},{1,5},{2,6},{3,7},{4,0},{5,1},{6,2},{7,3},{8,12},{9,13},{10,... | collective-permute-start | bytes 4718600 | tf_op jit(solution)/shard_map/ppermute | solution.py:14
Sparse Core Ops, SparseCore 0:
  9.8 29.2 all-gather.4
  40.9 35.1 all-gather.2
  88.7 43.8 reduce-scatter.1
